TPU v7x, 32 devices: a whole 2x2x4 slice. The times are simulated.
32 devices in a mesh: grp: 4 (over z), dp: 2 (over x), tp: 4 (over y, core).
Axes of the slice: x: 2, y: 2, z: 4, core: 2. Of those that a mesh axis runs over, the one named last changes fastest.
Arguments:
- hidden_last: bfloat16 [128, 5120], P(('grp', 'dp')), may hold values from -6 to 6
- gain: float32 [5120], replicated, may hold values from 0.25 to 1.75
- w_query: bfloat16 [5120, 2560], P('dp', 'tp'), may hold values from -0.078125 to 0.078125
- w_key: bfloat16 [5120, 512], P('dp', 'tp'), may hold values from -0.078125 to 0.078125
- w_value: bfloat16 [5120, 512], P('dp', 'tp'), may hold values from -0.078125 to 0.078125
- w_out: bfloat16 [2560, 5120], P('tp'), may hold values from -0.125 to 0.125
- cache_keys: bfloat16 [128, 128, 512], P(('grp', 'dp'), None, 'tp'), may hold values from -6 to 6
- cache_values: bfloat16 [128, 128, 512], P(('grp', 'dp'), None, 'tp'), may hold values from -6 to 6
- cache_lengths: int32 [128], P(('grp', 'dp')), may hold values from 1 to 128
- reward_vec: float32 [5120], replicated, may hold values from -0.078125 to 0.078125
- response_counts: int32 [128], P('grp'), may hold values from 4 to 16
- assignment: int32 [128], P('grp'), may hold values from 0 to 1, as said below
- responses: bfloat16 [128, 16, 5120], P(('grp', 'dp'), None, 'tp'), may hold values from -6 to 6
- cotangent: bfloat16 [128, 16, 5120], P(('grp', 'dp'), None, 'tp'), may hold values from -6 to 6
Outputs:
- decoded: bfloat16 [128, 5120], P(('grp', 'dp'))
- advantage: float32 [128], P(('grp', 'dp'))
- layer_out: bfloat16 [128, 16, 5120], P(('grp', 'dp'), None, 'tp')
- grad_query: float32 [5120, 2560], P('dp', 'tp')
- grad_key: float32 [5120, 512], P('dp', 'tp')
- grad_value: float32 [5120, 512], P('dp', 'tp')
Inputs may be any that keep to these rules, and one draw needn't show every extreme that they name: `assignment`: within each group, every training shard receives exactly 16 rows, and from the 16 rows of one device at most 10 rows go to one training shard; that most is reached for some shard in every group.
All inputs are finite; a program needn't handle non-finite values.
Results may differ from a plain program's by a relative error of at most 0.025.
Values may be sent and summed in bfloat16 or wider, within the bound.
A program may use at most 128 MiB of HBM per device.

v0:
```python
import jax
import jax.numpy as jnp
from jax import lax
from jax.sharding import PartitionSpec as P

HEAD_DIM = 128
STEPS = 2


def norm_rows(values, gain):
    wide = values.astype(jnp.float32)
    meansq = jnp.mean(wide * wide, axis=-1, keepdims=True)
    return (wide * lax.rsqrt(meansq + 1e-06) * gain).astype(jnp.bfloat16)


def rounded(values):
    return lax.optimization_barrier(values.astype(jnp.bfloat16)).astype(jnp.float32)


def decode_attend(query, cache_k, cache_v, lengths, new_k, new_v):
    rows_n = query.shape[0]
    slots = cache_k.shape[1]
    kv_n = cache_k.shape[2] // HEAD_DIM
    per_kv = query.shape[1] // cache_k.shape[2]
    scale = 1.0 / HEAD_DIM**0.5
    quer = query.reshape(rows_n, kv_n, per_kv, HEAD_DIM)
    keys_c = cache_k.reshape(rows_n, slots, kv_n, HEAD_DIM)
    vals_c = cache_v.reshape(rows_n, slots, kv_n, HEAD_DIM)
    keys_n = new_k.reshape(rows_n, -1, kv_n, HEAD_DIM)
    vals_n = new_v.reshape(rows_n, -1, kv_n, HEAD_DIM)
    score_c = (
        jnp.einsum("rkgd,rckd->rkgc", quer, keys_c, preferred_element_type=jnp.float32) * scale
    )
    score_n = (
        jnp.einsum("rkgd,rnkd->rkgn", quer, keys_n, preferred_element_type=jnp.float32) * scale
    )
    live = (jnp.arange(slots, dtype=jnp.int32)[None, :] < lengths[:, None])[:, None, None, :]
    score_c = jnp.where(live, score_c, -1e30)
    scores = jnp.concatenate([score_c, score_n], axis=-1)
    expo = jnp.exp(scores)
    weights = (expo / jnp.sum(expo, axis=-1, keepdims=True)).astype(jnp.bfloat16)
    context = jnp.einsum(
        "rkgc,rckd->rkgd", weights[..., :slots], vals_c, preferred_element_type=jnp.float32
    )
    context = context + jnp.einsum(
        "rkgn,rnkd->rkgd", weights[..., slots:], vals_n, preferred_element_type=jnp.float32
    )
    return context.reshape(rows_n, -1).astype(jnp.bfloat16)


def attend(query, keys, values, counts):
    rows_n = counts.shape[0]
    tokens = query.shape[0]
    length = tokens // rows_n
    kv_n = keys.shape[1] // HEAD_DIM
    per_kv = query.shape[1] // keys.shape[1]
    scale = 1.0 / HEAD_DIM**0.5
    quer = query.reshape(rows_n, length, kv_n, per_kv, HEAD_DIM).astype(jnp.float32)
    keyf = keys.reshape(rows_n, length, kv_n, HEAD_DIM).astype(jnp.float32)
    valf = values.reshape(rows_n, length, kv_n, HEAD_DIM).astype(jnp.float32)
    scores = jnp.einsum("rikgd,rjkd->rkgij", quer, keyf) * scale
    slot = jnp.arange(length, dtype=jnp.int32)
    causal = (slot[None, :] <= slot[:, None])[None, :, :]
    inside = slot[None, None, :] < counts[:, None, None]
    mask = (causal & inside)[:, None, None, :, :]
    scores = jnp.where(mask, scores, -1e30)
    expo = jnp.exp(scores)
    weights = (
        (expo / jnp.sum(expo, axis=-1, keepdims=True)).astype(jnp.bfloat16).astype(jnp.float32)
    )
    context = jnp.einsum("rkgij,rjkd->rikgd", weights, valf)
    return context.reshape(tokens, -1).astype(jnp.bfloat16)


def slot_valid(counts, length):
    slot = jnp.arange(length, dtype=jnp.int32)
    return (slot[None, :] < counts[:, None]).reshape(-1)


def exclusive_rank(labels, classes):
    onehot = (labels[:, None] == jnp.arange(classes, dtype=jnp.int32)[None, :]).astype(jnp.int32)
    return jnp.sum((jnp.cumsum(onehot, axis=0) - onehot) * onehot, axis=1)


def on_device(
    hidden_last,
    gain,
    w_query,
    w_key,
    w_value,
    w_out,
    cache_keys,
    cache_values,
    cache_lengths,
    reward_vec,
    response_counts,
    assignment,
    responses,
    cotangent,
):
    query_full, key_full, value_full = (
        lax.all_gather(w_query, "dp", axis=0, tiled=True),
        lax.all_gather(w_key, "dp", axis=0, tiled=True),
        lax.all_gather(w_value, "dp", axis=0, tiled=True),
    )
    state = hidden_last
    keys_new = []
    values_new = []
    for step in range(STEPS):
        normed = norm_rows(state, gain)
        query = jnp.dot(normed, query_full, preferred_element_type=jnp.float32).astype(jnp.bfloat16)
        keys_new.append(
            jnp.dot(normed, key_full, preferred_element_type=jnp.float32).astype(jnp.bfloat16)
        )
        values_new.append(
            jnp.dot(normed, value_full, preferred_element_type=jnp.float32).astype(jnp.bfloat16)
        )
        context = decode_attend(
            query,
            cache_keys,
            cache_values,
            cache_lengths,
            jnp.stack(keys_new, 1),
            jnp.stack(values_new, 1),
        )
        partial_out = jnp.dot(context, w_out, preferred_element_type=jnp.float32)
        state = (
            state.astype(jnp.float32)
            + lax.psum(partial_out.astype(jnp.bfloat16), "tp").astype(jnp.float32)
        ).astype(jnp.bfloat16)
    reward = jnp.sum(state.astype(jnp.float32) * reward_vec, axis=-1)
    total, squares = lax.psum((jnp.sum(reward), jnp.sum(reward * reward)), "dp")
    shards = lax.axis_size("dp")
    rows_dev = reward.shape[0]
    members = rows_dev * shards
    mean = total / members
    spread = squares / members - mean * mean
    advantage = (reward - mean) / jnp.sqrt(spread + 1e-05)
    adv_short = advantage.astype(jnp.bfloat16)
    myself = lax.axis_index("dp")
    group_rows = assignment.shape[0]
    positions = jnp.arange(group_rows, dtype=jnp.int32)
    owner_rank = exclusive_rank(assignment, shards)
    wanted = (assignment[None, :] == myself) & (
        owner_rank[None, :] == jnp.arange(rows_dev, dtype=jnp.int32)[:, None]
    )
    chosen = jnp.sum(jnp.where(wanted, positions[None, :], 0), axis=1)
    every_row, every_adv = (
        lax.all_gather(responses, "dp", axis=0, tiled=True),
        lax.all_gather(adv_short, "dp", axis=0, tiled=True),
    )
    mine = jnp.take(every_row, chosen, axis=0)
    my_adv = jnp.take(every_adv, chosen)
    length = mine.shape[1]
    tokens = mine.shape[0] * length
    local_in = mine.reshape(tokens, -1)
    local_cot = cotangent.reshape(tokens, -1)
    full_in, full_cot = (
        lax.all_gather(local_in, "tp", axis=1, tiled=True),
        lax.all_gather(local_cot, "tp", axis=1, tiled=True),
    )
    normed = norm_rows(full_in, gain)
    query = jnp.dot(normed, query_full, preferred_element_type=jnp.float32).astype(jnp.bfloat16)
    keys = jnp.dot(normed, key_full, preferred_element_type=jnp.float32).astype(jnp.bfloat16)
    values = jnp.dot(normed, value_full, preferred_element_type=jnp.float32).astype(jnp.bfloat16)
    counts = jnp.take(response_counts, chosen)
    valid = slot_valid(counts, length)
    context, pull = jax.vjp(lambda a, b, c: attend(a, b, c, counts), query, keys, values)
    partial_out = jnp.dot(context, w_out, preferred_element_type=jnp.float32)
    layer = (
        local_in.astype(jnp.float32)
        + lax.psum_scatter(
            partial_out.astype(jnp.bfloat16), "tp", scatter_dimension=1, tiled=True
        ).astype(jnp.float32)
    ).astype(jnp.bfloat16)
    token_weight = jnp.repeat(my_adv.astype(jnp.float32), length) * valid.astype(jnp.float32)
    upstream = (token_weight[:, None] * full_cot.astype(jnp.float32)).astype(jnp.bfloat16)
    d_context = lax.dot_general(
        upstream, w_out, (((1,), (1,)), ((), ())), preferred_element_type=jnp.float32
    ).astype(jnp.bfloat16)
    d_query, d_key, d_value = pull(d_context)
    block_rows = lax.all_to_all(normed, "dp", split_axis=1, concat_axis=0, tiled=True)
    width = block_rows.shape[1]
    empty_q = jnp.zeros((width, d_query.shape[1]), jnp.float32)
    empty_k = jnp.zeros((width, d_key.shape[1]), jnp.float32)
    empty_v = jnp.zeros((width, d_value.shape[1]), jnp.float32)
    pieces = (
        lax.all_gather(d_query, "dp", axis=0, tiled=True),
        lax.all_gather(d_key, "dp", axis=0, tiled=True),
        lax.all_gather(d_value, "dp", axis=0, tiled=True),
    )
    span = pieces[0].shape[0]
    count = span // tokens
    totals = list((empty_q, empty_k, empty_v))
    for member in range(count):
        left = block_rows[member * tokens : (member + 1) * tokens]
        for which in range(3):
            right = pieces[which][member * tokens : (member + 1) * tokens]
            term = lax.dot_general(
                left, right, (((0,), (0,)), ((), ())), preferred_element_type=jnp.float32
            )
            totals[which] = totals[which] + rounded(term)
    shard_q, shard_k, shard_v = tuple(totals)
    grad_q, grad_k, grad_v = (
        lax.psum(shard_q.astype(jnp.bfloat16), "grp").astype(jnp.float32),
        lax.psum(shard_k.astype(jnp.bfloat16), "grp").astype(jnp.float32),
        lax.psum(shard_v.astype(jnp.bfloat16), "grp").astype(jnp.float32),
    )
    return (state, advantage, layer.reshape(mine.shape[0], length, -1), grad_q, grad_k, grad_v)


def solution(mesh):
    return jax.shard_map(
        on_device,
        mesh=mesh,
        in_specs=(
            P(("grp", "dp"), None),
            P(),
            P("dp", "tp"),
            P("dp", "tp"),
            P("dp", "tp"),
            P("tp", None),
            P(("grp", "dp"), None, "tp"),
            P(("grp", "dp"), None, "tp"),
            P(("grp", "dp")),
            P(),
            P("grp"),
            P("grp"),
            P(("grp", "dp"), None, "tp"),
            P(("grp", "dp"), None, "tp"),
        ),
        out_specs=(
            P(("grp", "dp"), None),
            P(("grp", "dp")),
            P(("grp", "dp"), None, "tp"),
            P("dp", "tp"),
            P("dp", "tp"),
            P("dp", "tp"),
        ),
        check_vma=False,
    )
```

profile of v0, /device:TPU:0, one launch (start us, length us, event | category | flops | bytes accessed | tf_op | source)
XLA Modules:
  0.0 569.9 jit_solution(5665463674847834380)
XLA Ops:
  7.3 0.7 all-gather.9.cloned.1.call-update
  8.0 0.7 all-gather.11.cloned.1.call-update
  8.7 0.7 all-gather.7.cloned.1.call-update
  9.7 26.9 %all-gather.9.cloned.1.call-done = bf16[5120,128]{1,0:T(8,128)(2,1)} async-done(((bf16[2560,128]{1,0:T(8,128)(2,1)}), bf16[5120,128]{1,0:T(8,128)(2,1)}) %all-gather.9.cloned.1.call-update) | async-done | bytes 1310736 | tf_op jit(solution)/shard_map/all_gather | solution.py:103
  36.6 1.6 convolution_convert_fusion.20
  38.2 24.2 %all-gather.11.cloned.1.call-done = bf16[5120,128]{1,0:T(8,128)(2,1)} async-done(((bf16[2560,128]{1,0:T(8,128)(2,1)}), bf16[5120,128]{1,0:T(8,128)(2,1)}) %all-gather.11.cloned.1.call-update) | async-done | bytes 1310736 | tf_op jit(solution)/shard_map/all_gather | solution.py:104
  62.4 1.6 fusion.68
  64.0 83.2 %all-gather.7.cloned.1.call-done = bf16[5120,640]{1,0:T(8,128)(2,1)} async-done(((bf16[2560,640]{1,0:T(8,128)(2,1)}), bf16[5120,640]{1,0:T(8,128)(2,1)}) %all-gather.7.cloned.1.call-update) | async-done | bytes 6553616 | tf_op jit(solution)/shard_map/all_gather | solution.py:102
  147.2 3.8 convolution_convert_fusion.16
  152.7 4.5 convolution_convert_fusion.2
  157.3 0.5 all-gather.13.cloned.1.call-update
  158.4 0.6 dynamic-slice
  159.6 29.7 %all-reduce.7.cloned.1.call-done = bf16[16,5120]{1,0:T(8,128)(2,1)} async-done(((bf16[16,5120]{1,0:T(8,128)(2,1)}), bf16[16,5120]{1,0:T(8,128)(2,1)}) %all-reduce.7.cloned.1.call-update) | async-done | bytes 163856 | tf_op jit(solution)/shard_map/psum | solution.py:129
  189.3 1.1 fusion.26
  190.4 1.0 fusion.28
  191.4 4.5 convolution_convert_fusion.15
  196.0 0.9 reshape.456
  196.8 1.0 fusion.71
  198.4 1.0 copy.123
  200.7 4.5 convolution_convert_fusion.1
  205.3 9.6 %all-gather.13.cloned.1.call-done = bf16[32,16,1280]{2,1,0:T(8,128)(2,1)} async-done(((bf16[16,16,1280]{2,1,0:T(8,128)(2,1)}), bf16[32,16,1280]{2,1,0:T(8,128)(2,1)}) %all-gather.13.cloned.1.call-update) | async-done | bytes 1310736 | tf_op jit(solution)/shard_map/all_gather | solution.py:149
  215.0 1.9 gather_fusion
  216.9 32.8 %all-reduce.9.cloned.1.call-done = bf16[16,5120]{1,0:T(8,128)(2,1)} async-done(((bf16[16,5120]{1,0:T(8,128)(2,1)}), bf16[16,5120]{1,0:T(8,128)(2,1)}) %all-reduce.9.cloned.1.call-update) | async-done | bytes 163856 | tf_op jit(solution)/shard_map/psum | solution.py:129
  249.7 2.3 fusion.36
  251.9 0.6 multiply_reduce_fusion
  252.5 5.5 all-reduce.1
  260.7 0.5 fusion.66
  261.4 4.9 all-reduce
  266.3 0.7 gather_fusion.2
  267.2 1.0 bitcast_select_fusion
  268.3 0.7 all-gather.17.cloned.1.call-update
  269.2 0.7 gather_fusion.1
  270.2 23.7 %all-gather.15.cloned.1.call-done = bf16[256,5120]{1,0:T(8,128)(2,1)} async-done(((bf16[256,1280]{1,0:T(8,128)(2,1)}), bf16[256,5120]{1,0:T(8,128)(2,1)}) %all-gather.15.cloned.1.call-update) | async-done | bytes 2621456 | tf_op jit(solution)/shard_map/all_gather | solution.py:159
  293.9 2.5 fusion
  296.4 0.8 fusion.2
  297.2 5.1 convolution_convert_fusion.11
  302.3 0.4 reshape.461
  302.7 2.7 convolution_convert_fusion.13
  305.4 0.8 fusion.69
  306.2 0.8 convolution_convert_fusion.14
  307.5 6.6 %convolution_convert_fusion = bf16[256,5120]{1,0:T(8,128)(2,1)} fusion(bf16[640,5120]{1,0:T(8,128)(2,1)} %param.19, bf16[32,8,5,128]{3,2,1,0:T(8,128)(2,1)S(1)} %bitcast.188), kind=kOutput, calls=%fused_computation.6 | convolution fusion | flops 1679032320 | bytes 9502720 | tf_op jit(solution)/shard_map/dot_general | solution.py:169
  314.2 6.9 %all-gather.17.cloned.1.call-done = bf16[256,5120]{1,0:T(8,128)(2,1)} async-done(((bf16[256,1280]{1,0:T(8,128)(2,1)}), bf16[256,5120]{1,0:T(8,128)(2,1)}) %all-gather.17.cloned.1.call-update) | async-done | bytes 2621456 | tf_op jit(solution)/shard_map/all_gather | solution.py:160
  321.0 5.9 %fusion.6 = bf16[256,640]{1,0:T(8,128)(2,1)S(1)} fusion(bf16[640,5120]{1,0:T(8,128)(2,1)} %param.19, bf16[256,5120]{1,0:T(8,128)(2,1)} %all-gather.17.cloned.1.call-done, f32[256]{0:T(256)S(1)} %mul.176), kind=kOutput, calls=%fused_computation.29 | convolution fusion | flops 1681817600 | bytes 9503744 | tf_op jit(solution)/shard_map/dot_general | solution.py:178
  327.3 1.7 copy.184
  329.0 4.2 all-to-all-start
  333.5 1.9 fusion.21
  335.5 1.5 convolution_convert_fusion.12
  337.6 28.2 %all_gather.38 = bf16[512,128]{1,0:T(8,128)(2,1)S(1)} all-gather(bf16[256,128]{1,0:T(8,128)(2,1)S(1)} %bitcast.195), channel_id=1, replica_groups=mesh['grp'=4,'dp'=2,'tp'=4] {'dp'}, dimensions={0}, use_global_device_ids=true | all-gather | bytes 196608 | tf_op jit(solution)/shard_map/all_gather | solution.py:189
  366.1 4.9 all_gather.39
  371.0 8.6 %all_gather.37 = bf16[512,640]{1,0:T(8,128)(2,1)} all-gather(bf16[256,640]{1,0:T(8,128)(2,1)S(1)} %bitcast.185), channel_id=1, replica_groups=mesh['grp'=4,'dp'=2,'tp'=4] {'dp'}, dimensions={0}, use_global_device_ids=true | all-gather | bytes 983040 | tf_op jit(solution)/shard_map/all_gather | solution.py:188
  379.6 0.6 convolution_convert_fusion.8
  380.2 0.6 convolution_convert_fusion.7
  380.8 0.6 convolution_convert_fusion.6
  381.3 0.6 convolution_convert_fusion.5
  381.9 1.2 convolution_convert_fusion.4
  383.1 1.2 convolution_convert_fusion.3
  384.4 1.5 add_convert_fusion.1
  385.8 2.6 add_convert_fusion
  388.5 1.0 copy-done.9
  389.5 2.2 add_convert_fusion.3
  391.7 163.8 %all-reduce.11.cloned.1.call-done = (bf16[2560,640]{1,0:T(8,128)(2,1)}, bf16[2560,128]{1,0:T(8,128)(2,1)}, bf16[2560,128]{1,0:T(8,128)(2,1)}) async-done(((bf16[2560,640]{1,0:T(8,128)(2,1)}, bf16[2560,128]{1,0:T(8,128)(2,1)}, bf16[2560,128]{1,0:T(8,128)(2,1)}), (bf16[2560,640]{1,0:T(8,128)(2,1)}, bf16[2560,128]{1,0:T(8,128)(2,1)}, bf16[2560,128]{1,0:T(8,128)(2,1)})) %all-reduce.11.cloned.1.call-update) | async-done | bytes 4587536 | tf_op jit(solution)/shard_map/psum | solution.py:205
  555.5 5.3 convert_element_type.283
  560.8 1.1 convert_element_type.290
  561.9 1.1 convert_element_type.299
  (149 shorter events, 7.4 us)
Async XLA Ops:
  7.2 144.2 %copy-start = (bf16[16,128,128]{2,1,0:T(8,128)(2,1)S(1)}, bf16[16,128,128]{2,1,0:T(8,128)(2,1)}, u32[]{:S(2)}) copy-start(bf16[16,128,128]{2,1,0:T(8,128)(2,1)} %param.20) | copy-start | bytes 1572868
  7.2 2.3 copy-start.7
  7.2 2.5 copy-start.31
  7.2 29.3 %copy-start.22 = (f32[5120]{0:T(1024)S(1)}, f32[5120]{0:T(1024)}, u32[]{:S(2)}) copy-start(f32[5120]{0:T(1024)} %param.15) | copy-start | bytes 61444
  7.2 29.3 %all-gather.9.cloned.1.call-start = ((), (), s32[]{:S(2)}) async-start(), calls=%async_computation.3 | async-start | bytes 1966080 | tf_op jit(solution)/shard_map/all_gather | solution.py:103
  7.9 54.4 %all-gather.11.cloned.1.call-start = ((), (), s32[]{:S(2)}) async-start(), calls=%async_computation.4 | async-start | bytes 1966080 | tf_op jit(solution)/shard_map/all_gather | solution.py:104
  8.7 138.5 %all-gather.7.cloned.1.call-start = ((), (), s32[]{:S(2)}) async-start(), calls=%async_computation.2 | async-start | bytes 9830400 | tf_op jit(solution)/shard_map/all_gather | solution.py:102
  9.4 179.9 %all-reduce.7.cloned.1.call-start = ((), (), s32[]{:S(2)}) async-start(), calls=%async_computation.5 | async-start | bytes 327680 | tf_op jit(solution)/shard_map/psum | solution.py:129
  151.1 1.3 copy-start.11
  152.7 5.2 copy-start.30
  152.7 5.7 copy-start.34
  157.2 57.7 %all-gather.13.cloned.1.call-start = ((), (), s32[]{:S(2)}) async-start(), calls=%async_computation.7 | async-start | bytes 1966080 | tf_op jit(solution)/shard_map/all_gather | solution.py:149
  157.8 91.8 %all-reduce.9.cloned.1.call-start = ((), (), s32[]{:S(2)}) async-start(), calls=%async_computation.6 | async-start | bytes 327680 | tf_op jit(solution)/shard_map/psum | solution.py:129
  158.3 31.0 %copy-start.32 = (s32[16]{0:T(128)}, s32[16]{0:T(128)S(1)}, u32[]{:S(2)}) copy-start(s32[16]{0:T(128)S(1)} %select_reduce_fusion.1) | copy-start | bytes 196
  191.4 6.4 %copy-start.3 = (bf16[5120,128]{1,0:T(8,128)(2,1)S(1)}, bf16[5120,128]{1,0:T(8,128)(2,1)}, u32[]{:S(2)}) copy-start(bf16[5120,128]{1,0:T(8,128)(2,1)} %all-gather.9.cloned.1.call-done) | copy-start | bytes 3932164
  196.0 4.0 copy-start.4
  198.1 2.1 copy-start.12
  200.7 49.0 %copy-start.13 = (bf16[16,5120]{1,0:T(8,128)(2,1)S(1)}, bf16[16,5120]{1,0:T(8,128)(2,1)}, u32[]{:S(2)}) copy-start(bf16[16,5120]{1,0:T(8,128)(2,1)} %all-reduce.7.cloned.1.call-done) | copy-start | bytes 491524
  200.7 49.0 %copy-start.29 = (f32[5120]{0:T(1024)S(1)}, f32[5120]{0:T(1024)}, u32[]{:S(2)}) copy-start(f32[5120]{0:T(1024)} %param.23) | copy-start | bytes 61444
  205.2 61.8 %copy-start.33 = (s32[16]{0:T(128)S(1)}, s32[16]{0:T(128)}, u32[]{:S(2)}) copy-start(s32[16]{0:T(128)} %copy-done.32) | copy-start | bytes 196
  205.3 63.9 %copy-start.2 = (s32[32]{0:T(128)S(1)}, s32[32]{0:T(128)}, u32[]{:S(2)}) copy-start(s32[32]{0:T(128)} %param.24) | copy-start | bytes 388
  205.3 88.6 %all-gather.15.cloned.1.call-start = ((), (), s32[]{:S(2)}) async-start(), calls=%async_computation.8 | async-start | bytes 3276800 | tf_op jit(solution)/shard_map/all_gather | solution.py:159
  216.9 79.5 %copy-start.8 = (bf16[16,16,1280]{2,1,0:T(8,128)(2,1)}, bf16[16,16,1280]{2,1,0:T(8,128)(2,1)S(1)}, u32[]{:S(2)}) copy-start(bf16[16,16,1280]{2,1,0:T(8,128)(2,1)S(1)} %gather_fusion) | copy-start | bytes 1966084
  268.2 52.8 %all-gather.17.cloned.1.call-start = ((), (), s32[]{:S(2)}) async-start(), calls=%async_computation.10 | async-start | bytes 3276800 | tf_op jit(solution)/shard_map/all_gather | solution.py:160
  269.0 119.5 %reduce-scatter.2.cloned.1.call-start = ((), (), s32[]{:S(2)}) async-start(), calls=%async_computation.9 | async-start | bytes 3276800 | tf_op jit(solution)/shard_map/reduce_scatter | solution.py:172
  270.2 35.1 %copy-start.27 = (pred[16,16,16]{1,2,0:T(8,128)(4,1)}, pred[16,16,16]{1,2,0:T(8,128)(4,1)S(1)}, u32[]{:S(2)}) copy-start(pred[16,16,16]{1,2,0:T(8,128)(4,1)S(1)} %broadcast_and_fusion) | copy-start | bytes 12292
  293.9 2.5 copy-start.6
  302.7 4.4 copy-start.20
  302.7 3.5 copy-start.5
  305.3 2.0 copy-start.23
  306.2 1.2 copy-start.16
  306.2 1.2 copy-start.25
  327.3 6.2 %copy-start.14 = (bf16[16,16,1,5,128]{4,3,1,0,2:T(8,128)(2,1)}, bf16[16,16,1,5,128]{4,3,1,0,2:T(8,128)(2,1)S(1)}, u32[]{:S(2)}) copy-start(bf16[16,16,1,5,128]{4,3,1,0,2:T(8,128)(2,1)S(1)} %reshape.465) | copy-start | bytes 983044
  329.0 4.5 copy-start.26
  329.0 6.4 %copy-start.24 = (bf16[256,128]{1,0:T(8,128)(2,1)S(1)}, bf16[256,128]{1,0:T(8,128)(2,1)}, u32[]{:S(2)}) copy-start(bf16[256,128]{1,0:T(8,128)(2,1)} %copy-done.23) | copy-start | bytes 196612
  329.0 6.4 %copy-start.28 = (pred[16,16,16]{1,2,0:T(8,128)(4,1)S(1)}, pred[16,16,16]{1,2,0:T(8,128)(4,1)}, u32[]{:S(2)}) copy-start(pred[16,16,16]{1,2,0:T(8,128)(4,1)} %copy-done.27) | copy-start | bytes 12292
  329.0 50.6 %all-to-all-start = ((bf16[256,2,2560]{2,0,1:T(8,128)(2,1)}), bf16[256,2,2560]{2,0,1:T(8,128)(2,1)S(1)}, u32[]{:S(2)}, u32[]{:S(2)}) async-start(bf16[256,2,2560]{2,0,1:T(8,128)(2,1)} %bitcast.181), calls=%async_computation.1 | async-start | bytes 5242880 | tf_op jit(solution)/shard_map/all_to_all | solution.py:182
  333.2 222.3 %all-reduce.11.cloned.1.call-start = ((), (), s32[]{:S(2)}) async-start(), calls=%async_computation.11 | async-start | bytes 9175040 | tf_op jit(solution)/shard_map/psum | solution.py:205
  335.4 1.8 copy-start.17
  335.4 1.8 copy-start.21
  337.0 28.7 %copy-start.15 = (bf16[16,16,1,5,128]{4,3,1,0,2:T(8,128)(2,1)S(1)}, bf16[16,16,1,5,128]{4,3,1,0,2:T(8,128)(2,1)}, u32[]{:S(2)}) copy-start(bf16[16,16,1,5,128]{4,3,1,0,2:T(8,128)(2,1)} %copy-done.14) | copy-start | bytes 983044
  380.2 1.7 copy-start.10
  388.4 1.1 copy-start.9
  555.5 5.3 copy-start.19
  555.5 6.4 %copy-start.18 = (bf16[2560,128]{1,0:T(8,128)(2,1)S(1)}, bf16[2560,128]{1,0:T(8,128)(2,1)}, u32[]{:S(2)}) copy-start(bf16[2560,128]{1,0:T(8,128)(2,1)} %get-tuple-element.12) | copy-start | bytes 1966084
  555.5 7.6 %copy-start.1 = (bf16[16,128,128]{2,1,0:T(8,128)(2,1)S(1)}, bf16[16,128,128]{2,1,0:T(8,128)(2,1)}, u32[]{:S(2)}) copy-start(bf16[16,128,128]{2,1,0:T(8,128)(2,1)} %param.20) | copy-start | bytes 1572868
Sparse Core Ops, SparseCore 0:
  9.6 26.9 all-gather.8
  38.1 24.2 all-gather.10
  63.9 83.2 all-gather.6
  157.4 31.9 all-reduce.6
  190.7 24.2 all-gather.12
  217.7 31.9 all-reduce.8
  268.3 25.5 all-gather.14
  295.5 25.5 all-gather.16
  323.6 34.3 reduce-scatter.1
  388.6 166.8 all-reduce.10
where the time goes:
time: 571 us; the launch traced here: 570 us
  waiting for transfers between devices  404 us (71%)
  matrix products  54.5 us (10%)
  blocking collectives  52.2 us (9%)
  other arithmetic  24.9 us (4%)
  between operations  18.2 us (3%)
  local copies, waits for them, and re-layouts  11 us (2%)
    psum x1, waiting for transfers between devices, on_device(): lax.psum(shard_q.astype(jnp.bfloat16), 'grp').astype(jnp.float32)  164 us
    all_gather x1, waiting for transfers between devices, on_device(): lax.all_gather(w_query, 'dp', axis=0, tiled=True)  83.2 us
    psum x2, waiting for transfers between devices, on_device(): lax.psum(partial_out.astype(jnp.bfloat16), 'tp').astype(jnp.float32)  62.5 us
    all_gather x1, blocking collectives, on_device(): lax.all_gather(d_key, 'dp', axis=0, tiled=True)  28.2 us
    all_gather x1, waiting for transfers between devices, on_device(): lax.all_gather(w_key, 'dp', axis=0, tiled=True)  26.9 us
    all_gather x1, waiting for transfers between devices, on_device(): lax.all_gather(w_value, 'dp', axis=0, tiled=True)  24.2 us
    all_gather x1, waiting for transfers between devices, on_device(): lax.all_gather(local_in, 'tp', axis=1, tiled=True)  23.7 us
    dot_general x3, matrix products, on_device(): partial_out = jnp.dot(context, w_out, preferred_element_type=jnp.float32)  15.7 us
  transfers between devices with their start and end apart: 11, of which 9 were waited for; matrix products, arithmetic and copies ran while one was open for 12% of the time, Pallas kernels for 0%

commit v1 on v0

v1 whole, which is shorter than its diff:
```python
import jax
import jax.numpy as jnp
from jax import lax
from jax.experimental import pallas as pl
from jax.experimental.pallas import tpu as pltpu
from jax.sharding import PartitionSpec as P

HEAD_DIM = 128
STEPS = 2


def norm_rows(values, gain):
    wide = values.astype(jnp.float32)
    meansq = jnp.mean(wide * wide, axis=-1, keepdims=True)
    return (wide * lax.rsqrt(meansq + 1e-06) * gain).astype(jnp.bfloat16)


def rounded(values):
    return lax.optimization_barrier(values.astype(jnp.bfloat16)).astype(jnp.float32)


def decode_attend(query, cache_k, cache_v, lengths, new_k, new_v):
    rows_n = query.shape[0]
    slots = cache_k.shape[1]
    kv_n = cache_k.shape[2] // HEAD_DIM
    per_kv = query.shape[1] // cache_k.shape[2]
    scale = 1.0 / HEAD_DIM**0.5
    quer = query.reshape(rows_n, kv_n, per_kv, HEAD_DIM)
    keys_c = cache_k.reshape(rows_n, slots, kv_n, HEAD_DIM)
    vals_c = cache_v.reshape(rows_n, slots, kv_n, HEAD_DIM)
    keys_n = new_k.reshape(rows_n, -1, kv_n, HEAD_DIM)
    vals_n = new_v.reshape(rows_n, -1, kv_n, HEAD_DIM)
    score_c = (
        jnp.einsum("rkgd,rckd->rkgc", quer, keys_c, preferred_element_type=jnp.float32) * scale
    )
    score_n = (
        jnp.einsum("rkgd,rnkd->rkgn", quer, keys_n, preferred_element_type=jnp.float32) * scale
    )
    live = (jnp.arange(slots, dtype=jnp.int32)[None, :] < lengths[:, None])[:, None, None, :]
    score_c = jnp.where(live, score_c, -1e30)
    scores = jnp.concatenate([score_c, score_n], axis=-1)
    expo = jnp.exp(scores)
    weights = (expo / jnp.sum(expo, axis=-1, keepdims=True)).astype(jnp.bfloat16)
    context = jnp.einsum(
        "rkgc,rckd->rkgd", weights[..., :slots], vals_c, preferred_element_type=jnp.float32
    )
    context = context + jnp.einsum(
        "rkgn,rnkd->rkgd", weights[..., slots:], vals_n, preferred_element_type=jnp.float32
    )
    return context.reshape(rows_n, -1).astype(jnp.bfloat16)


def attend(query, keys, values, counts):
    rows_n = counts.shape[0]
    tokens = query.shape[0]
    length = tokens // rows_n
    kv_n = keys.shape[1] // HEAD_DIM
    per_kv = query.shape[1] // keys.shape[1]
    scale = 1.0 / HEAD_DIM**0.5
    quer = query.reshape(rows_n, length, kv_n, per_kv, HEAD_DIM).astype(jnp.float32)
    keyf = keys.reshape(rows_n, length, kv_n, HEAD_DIM).astype(jnp.float32)
    valf = values.reshape(rows_n, length, kv_n, HEAD_DIM).astype(jnp.float32)
    scores = jnp.einsum("rikgd,rjkd->rkgij", quer, keyf) * scale
    slot = jnp.arange(length, dtype=jnp.int32)
    causal = (slot[None, :] <= slot[:, None])[None, :, :]
    inside = slot[None, None, :] < counts[:, None, None]
    mask = (causal & inside)[:, None, None, :, :]
    scores = jnp.where(mask, scores, -1e30)
    expo = jnp.exp(scores)
    weights = (
        (expo / jnp.sum(expo, axis=-1, keepdims=True)).astype(jnp.bfloat16).astype(jnp.float32)
    )
    context = jnp.einsum("rkgij,rjkd->rikgd", weights, valf)
    return context.reshape(tokens, -1).astype(jnp.bfloat16)


def slot_valid(counts, length):
    slot = jnp.arange(length, dtype=jnp.int32)
    return (slot[None, :] < counts[:, None]).reshape(-1)


def exclusive_rank(labels, classes):
    onehot = (labels[:, None] == jnp.arange(classes, dtype=jnp.int32)[None, :]).astype(jnp.int32)
    return jnp.sum((jnp.cumsum(onehot, axis=0) - onehot) * onehot, axis=1)


def exchange(axis, ident, gathers=(), swaps=()):
    members = lax.axis_size(axis)
    items = tuple(gathers) + tuple(swaps)
    total = len(items)

    def kernel(*refs):
        ins, outs = refs[:total], refs[total : 2 * total]
        send_sem, recv_sem, own_sem = refs[2 * total :]
        me = lax.axis_index(axis)
        peers = [lax.rem(me + off, members) for off in range(1, members)]
        barrier = pltpu.get_barrier_semaphore()
        for peer in peers:
            pl.semaphore_signal(
                barrier, inc=1, device_id={axis: peer}, device_id_type=pl.DeviceIdType.MESH
            )
        pl.semaphore_wait(barrier, members - 1)
        copies = []
        for at, peer in enumerate(peers):
            for which in range(total):
                source = ins[which] if which < len(gathers) else ins[which].at[peer]
                copy = pltpu.make_async_remote_copy(
                    src_ref=source,
                    dst_ref=outs[which].at[me],
                    send_sem=send_sem.at[which * (members - 1) + at],
                    recv_sem=recv_sem.at[which * (members - 1) + at],
                    device_id={axis: peer},
                    device_id_type=pl.DeviceIdType.MESH,
                )
                copy.start()
                copies.append(copy)
        for which in range(total):
            source = ins[which] if which < len(gathers) else ins[which].at[me]
            copy = pltpu.make_async_copy(source, outs[which].at[me], own_sem.at[which])
            copy.start()
            copies.append(copy)
        for copy in copies:
            copy.wait()

    shapes = [(members,) + item.shape for item in gathers] + [item.shape for item in swaps]
    sent = sum(
        2 * item.size * (members if at < len(gathers) else 1) for at, item in enumerate(items)
    )
    return pl.pallas_call(
        kernel,
        out_shape=[jax.ShapeDtypeStruct(sh, item.dtype) for sh, item in zip(shapes, items)],
        in_specs=[pl.BlockSpec(memory_space=pltpu.VMEM)] * total,
        out_specs=[pl.BlockSpec(memory_space=pltpu.VMEM)] * total,
        scratch_shapes=[
            pltpu.SemaphoreType.DMA((total * (members - 1),)),
            pltpu.SemaphoreType.DMA((total * (members - 1),)),
            pltpu.SemaphoreType.DMA((total,)),
        ],
        compiler_params=pltpu.CompilerParams(collective_id=ident, has_side_effects=True),
        cost_estimate=pl.CostEstimate(
            flops=sent * 1000, bytes_accessed=2 * sent, transcendentals=0
        ),
        name=f"exchange_{ident}",
    )(*items)


def side_by_side(parts):
    return jnp.moveaxis(parts, 0, 1).reshape(parts.shape[1], -1)


def cut(values, members):
    return jnp.moveaxis(values.reshape(values.shape[0], members, -1), 1, 0)


def project(rows, weights):
    return jnp.concatenate(
        [jnp.dot(rows, weight, preferred_element_type=jnp.float32) for weight in weights], axis=1
    )


def split_qkv(joined, weights):
    first = weights[0].shape[1]
    second = first + weights[1].shape[1]
    return joined[:, :first], joined[:, first:second], joined[:, second:]


def on_device(
    hidden_last,
    gain,
    w_query,
    w_key,
    w_value,
    w_out,
    cache_keys,
    cache_values,
    cache_lengths,
    reward_vec,
    response_counts,
    assignment,
    responses,
    cotangent,
):
    shards = lax.axis_size("dp")
    feats = lax.axis_size("tp")
    myself = lax.axis_index("dp")
    weights = (w_query, w_key, w_value)
    rows_dev, length, _ = responses.shape
    tokens = rows_dev * length
    group_rows = assignment.shape[0]

    positions = jnp.arange(group_rows, dtype=jnp.int32)
    place = assignment * rows_dev + exclusive_rank(assignment, shards)
    order = jnp.sum(jnp.where(place[None, :] == positions[:, None], positions[None, :], 0), axis=1)
    chosen = lax.dynamic_slice_in_dim(order, myself * rows_dev, rows_dev)

    (row_parts,) = exchange("tp", 0, gathers=(responses.reshape(tokens, -1),))
    own_normed = norm_rows(side_by_side(row_parts), gain)
    (block,) = exchange("dp", 1, swaps=(cut(own_normed, shards),))
    width = block.shape[-1]
    block = jnp.take(block.reshape(group_rows, length, width), order, axis=0)
    block = block.reshape(group_rows * length, width)
    share = group_rows * length // feats
    every_block = lax.all_gather(
        lax.dynamic_slice_in_dim(block, lax.axis_index("tp") * share, share),
        ("grp", "tp"),
        axis=0,
        tiled=True,
    )

    joined = project(block, weights).astype(jnp.bfloat16)
    mine_x = jnp.take(
        lax.all_gather(responses, "dp", axis=0, tiled=True), chosen, axis=0
    ).reshape(tokens, -1)
    (joined_parts,) = exchange("dp", 2, swaps=(joined.reshape(shards, tokens, -1),))
    joined = jnp.sum(joined_parts.astype(jnp.float32), axis=0).astype(jnp.bfloat16)
    query, keys, values = split_qkv(joined, weights)
    counts = jnp.take(response_counts, chosen)
    valid = slot_valid(counts, length)
    context, pull = jax.vjp(lambda a, b, c: attend(a, b, c, counts), query, keys, values)
    partial_out = jnp.dot(context, w_out, preferred_element_type=jnp.float32)
    layer = (
        mine_x.astype(jnp.float32)
        + lax.psum_scatter(
            partial_out.astype(jnp.bfloat16), "tp", scatter_dimension=1, tiled=True
        ).astype(jnp.float32)
    ).astype(jnp.bfloat16)

    local_cot = cotangent.reshape(tokens, -1) * valid.astype(jnp.bfloat16)[:, None]
    (cot_parts,) = exchange("tp", 3, gathers=(local_cot,))
    d_context = lax.dot_general(
        side_by_side(cot_parts),
        w_out,
        (((1,), (1,)), ((), ())),
        preferred_element_type=jnp.float32,
    ).astype(jnp.bfloat16)
    d_joined = jnp.concatenate(pull(d_context), axis=1)

    state = hidden_last
    keys_new = []
    values_new = []
    for step in range(STEPS):
        normed = norm_rows(state, gain)
        (pieces,) = exchange("dp", 4 + 3 * step, swaps=(cut(normed, shards),))
        part = project(pieces.reshape(group_rows, -1), weights)
        (parts,) = exchange("dp", 5 + 3 * step, swaps=(part.reshape(shards, rows_dev, -1),))
        step_q, step_k, step_v = split_qkv(
            jnp.sum(parts, axis=0).astype(jnp.bfloat16), weights
        )
        keys_new.append(step_k)
        values_new.append(step_v)
        step_context = decode_attend(
            step_q,
            cache_keys,
            cache_values,
            cache_lengths,
            jnp.stack(keys_new, 1),
            jnp.stack(values_new, 1),
        )
        step_out = jnp.dot(step_context, w_out, preferred_element_type=jnp.float32)
        (outs,) = exchange("tp", 6 + 3 * step, gathers=(step_out.astype(jnp.bfloat16),))
        state = (
            state.astype(jnp.float32) + jnp.sum(outs.astype(jnp.float32), axis=0)
        ).astype(jnp.bfloat16)
    reward = jnp.sum(state.astype(jnp.float32) * reward_vec, axis=-1, keepdims=True)
    (every_reward,) = exchange(
        "dp", 4 + 3 * STEPS, gathers=(jnp.broadcast_to(reward, (rows_dev, HEAD_DIM)),)
    )
    rewards = every_reward[:, :, 0].reshape(-1)
    mean = jnp.sum(rewards) / group_rows
    spread = jnp.sum(rewards * rewards) / group_rows - mean * mean
    every_adv = (rewards - mean) / jnp.sqrt(spread + 1e-05)
    advantage = lax.dynamic_slice_in_dim(every_adv, myself * rows_dev, rows_dev)
    my_adv = jnp.take(every_adv.astype(jnp.bfloat16), chosen).astype(jnp.float32)

    scaled = (jnp.repeat(my_adv, length)[:, None] * d_joined.astype(jnp.float32)).astype(
        jnp.bfloat16
    )
    every_d = lax.all_gather(scaled, ("grp", "dp"), axis=0, tiled=True)
    grad_q, grad_k, grad_v = (
        lax.dot_general(
            every_block, piece, (((0,), (0,)), ((), ())), preferred_element_type=jnp.float32
        )
        for piece in split_qkv(every_d, weights)
    )
    return (state, advantage, layer.reshape(rows_dev, length, -1), grad_q, grad_k, grad_v)


def solution(mesh):
    return jax.shard_map(
        on_device,
        mesh=mesh,
        in_specs=(
            P(("grp", "dp"), None),
            P(),
            P("dp", "tp"),
            P("dp", "tp"),
            P("dp", "tp"),
            P("tp", None),
            P(("grp", "dp"), None, "tp"),
            P(("grp", "dp"), None, "tp"),
            P(("grp", "dp")),
            P(),
            P("grp"),
            P("grp"),
            P(("grp", "dp"), None, "tp"),
            P(("grp", "dp"), None, "tp"),
        ),
        out_specs=(
            P(("grp", "dp"), None),
            P(("grp", "dp")),
            P(("grp", "dp"), None, "tp"),
            P("dp", "tp"),
            P("dp", "tp"),
            P("dp", "tp"),
        ),
        check_vma=False,
    )
```

time: 571 us -> 486 us (0.85)
  waiting for transfers between devices: 404 us -> 150 us
  Pallas kernels: 0 us -> 166 us
  blocking collectives: 52.2 us -> 0 us
  local copies, waits for them, and re-layouts: 11 us -> 40.7 us
  matrix products: 54.5 us -> 70.2 us
  other arithmetic: 24.9 us -> 37.5 us
    psum x3 -> x0, waiting for transfers between devices: 226 us -> none  [the longest x1 164 us: on_device(): lax.psum(shard_q.astype(jnp.bfloat16), 'grp').astype(jnp.float32)]
    pallas_call x0 -> x11, Pallas kernels: none -> 166 us  [exchange(): pl.pallas_call(kernel, out_shape=[jax.ShapeDtypeStruct(sh, item.dtype) fo...]
    all_gather x3 -> x0, blocking collectives: 41.7 us -> none  [the longest x1 28.2 us: on_device(): lax.all_gather(d_key, 'dp', axis=0, tiled=True)]
    dot_general x16 -> x15, matrix products: 31.4 us -> 52.5 us  [the longest x3 24 us: on_device(): lax.dot_general(every_block, piece, (((0,), (0,)), ((), ())), preferred_e...]
    all_gather x5 -> x2, waiting for transfers between devices: 165 us -> 150 us  [the longest x1 89.1 us: on_device(): lax.all_gather(lax.dynamic_slice_in_dim(block, lax.axis_index('tp') * sha...]
    convert_element_type x0 -> x3, local copies, waits for them, and re-layouts: none -> 11.9 us  [the longest x2 11.8 us: norm_rows(): wide = values.astype(jnp.float32)]
    all_gather x1, waiting for transfers between devices: 9.61 us -> 0.01 us  [on_device(): lax.all_gather(responses, 'dp', axis=0, tiled=True)]
    dot_general x3 -> x1, matrix products: 15.7 us -> 6.59 us  [on_device(): partial_out = jnp.dot(context, w_out, preferred_element_type=jnp.float32)]
  transfers between devices with their start and end apart: 11 -> 4, of which waited for: 9 -> 2; matrix products, arithmetic and copies ran while one was open for 12% -> 26% of each run, Pallas kernels for 0% -> 34%
where the time goes in v1:
time: 486 us; the launch traced here: 484 us
  Pallas kernels  166 us (34%)
  waiting for transfers between devices  150 us (31%)
  matrix products  70.2 us (14%)
  local copies, waits for them, and re-layouts  40.7 us (8%)
  other arithmetic  37.5 us (8%)
  between operations  18.6 us (4%)
    pallas_call x11, Pallas kernels, exchange(): pl.pallas_call(kernel, out_shape=[jax.ShapeDtypeStruct(sh, item.dtype) fo...  166 us
    all_gather x1, waiting for transfers between devices, on_device(): lax.all_gather(lax.dynamic_slice_in_dim(block, lax.axis_index('tp') * sha...  89.1 us
    all_gather x1, waiting for transfers between devices, on_device(): every_d = lax.all_gather(scaled, ('grp', 'dp'), axis=0, tiled=True)  60.6 us
    dot_general x3, matrix products, on_device(): lax.dot_general(every_block, piece, (((0,), (0,)), ((), ())), preferred_e...  24 us
    dot_general x9, matrix products, project(): jnp.dot(rows, weight, preferred_element_type=jnp.float32)  13.6 us
    convert_element_type x2, local copies, waits for them, and re-layouts, norm_rows(): wide = values.astype(jnp.float32)  11.8 us
  transfers between devices with their start and end apart: 4, of which 2 were waited for; matrix products, arithmetic and copies ran while one was open for 26% of the time, Pallas kernels for 34%

profile of v1, /device:TPU:0, one launch (start us, length us, event | category | flops | bytes accessed | tf_op | source)
XLA Modules:
  0.0 483.7 jit_solution(6164549682191265670)
XLA Ops:
  8.8 34.4 %exchange_0.1 = bf16[4,256,1280]{2,1,0:T(8,128)(2,1)} custom-call(bf16[256,1280]{1,0:T(8,128)(2,1)} %bitcast.224), custom_call_target="tpu_custom_call" | custom-call | flops 2621440000 | bytes 5242880 | tf_op jit(solution)/shard_map/exchange_0/pallas_call | solution.py:129
  43.3 4.7 convert_bitcast_fusion
  49.3 5.9 %copy.233 = f32[256,4,1280]{0,2,1:T(8,128)} copy(f32[256,4,1280]{2,0,1:T(8,128)} %convert_bitcast_fusion) | data formatting | bytes 10485760 | tf_op jit(solution)/shard_map/convert_element_type | solution.py:13
  55.2 5.9 %copy.234 = f32[256,2,2560]{2,0,1:T(8,128)} copy(f32[256,2,2560]{0,2,1:T(8,128)} %bitcast.208) | data formatting | bytes 10485760 | tf_op jit(solution)/shard_map/convert_element_type | solution.py:13
  61.1 4.7 fusion.3.refs_0_
  65.9 34.6 %exchange_1.1 = bf16[2,256,2560]{2,1,0:T(8,128)(2,1)} custom-call(bf16[2,256,2560]{2,1,0:T(8,128)(2,1)} %fusion.3.refs_0_), custom_call_target="tpu_custom_call" | custom-call | flops 2621440000 | bytes 5242880 | tf_op jit(solution)/shard_map/exchange_1/pallas_call | solution.py:129
  100.5 3.9 gather_fusion.1
  104.5 2.1 bitcast_select_fusion
  106.6 0.8 convolution_convert_fusion.7
  107.5 0.8 convolution_convert_fusion.8
  108.4 3.0 fusion.6
  112.0 1.2 gather_fusion.2
  115.2 2.1 pad_maximum_fusion.refs_0_
  117.3 14.4 %exchange_2.1 = bf16[2,256,896]{2,1,0:T(8,128)(2,1)} custom-call(bf16[2,256,896]{2,1,0:T(8,128)(2,1)} %pad_maximum_fusion.refs_0_), custom_call_target="tpu_custom_call" | custom-call | flops 917504000 | bytes 1835008 | tf_op jit(solution)/shard_map/exchange_2/pallas_call | solution.py:129
  131.7 2.2 reduce_sum.180
  133.9 1.7 slice.88
  135.7 2.1 reshape.530
  137.8 0.9 fusion.71
  138.7 1.8 fusion.72
  141.4 6.6 %convolution_convert_fusion = bf16[256,5120]{1,0:T(8,128)(2,1)} fusion(bf16[640,5120]{1,0:T(8,128)(2,1)} %param.19, bf16[32,8,5,128]{3,2,1,0:T(8,128)(2,1)S(1)} %bitcast.228), kind=kOutput, calls=%fused_computation.6 | convolution fusion | flops 1679032320 | bytes 9502720 | tf_op jit(solution)/shard_map/dot_general | solution.py:220
  149.2 6.0 %exchange_4.1 = bf16[2,16,2560]{2,1,0:T(8,128)(2,1)} custom-call(bf16[2,16,2560]{2,1,0:T(8,128)(2,1)} %bitcast.233), custom_call_target="tpu_custom_call" | custom-call | flops 163840000 | bytes 327680 | tf_op jit(solution)/shard_map/exchange_4/pallas_call | solution.py:129
  155.3 1.6 fusion.75
  156.8 1.4 fusion.74
  158.3 1.6 fusion.73
  160.5 5.7 %exchange_5.1 = f32[2,16,896]{2,1,0:T(8,128)} custom-call(f32[2,16,896]{2,1,0:T(8,128)} %bitcast.229), custom_call_target="tpu_custom_call" | custom-call | flops 57344000 | bytes 114688 | tf_op jit(solution)/shard_map/exchange_5/pallas_call | solution.py:129
  166.3 0.9 reduce_sum.165
  168.4 1.4 reshape.517
  169.8 0.9 fusion.60
  170.8 2.1 fusion.76
  172.9 1.7 copy.220
  175.3 1.0 select_bitcast_fusion.1
  177.2 1.6 copy.222
  178.9 1.3 fusion.17
  180.2 4.5 convolution_convert_fusion.2.refs_0_
  184.7 10.1 %exchange_6.1 = bf16[4,16,5120]{2,1,0:T(8,128)(2,1)} custom-call(bf16[16,5120]{1,0:T(8,128)(2,1)} %convolution_convert_fusion.2.refs_0_), custom_call_target="tpu_custom_call" | custom-call | flops 655360000 | bytes 1310720 | tf_op jit(solution)/shard_map/exchange_6/pallas_call | solution.py:129
  194.8 1.2 convert_reduce_fusion.1
  197.6 6.3 %exchange_7.1 = bf16[2,16,2560]{2,1,0:T(8,128)(2,1)} custom-call(bf16[2,16,2560]{2,1,0:T(8,128)(2,1)} %bitcast.234), custom_call_target="tpu_custom_call" | custom-call | flops 163840000 | bytes 327680 | tf_op jit(solution)/shard_map/exchange_7/pallas_call | solution.py:129
  203.9 1.4 fusion.79
  205.3 1.4 fusion.78
  206.7 1.6 fusion.77
  209.0 5.8 %exchange_8.1 = f32[2,16,896]{2,1,0:T(8,128)} custom-call(f32[2,16,896]{2,1,0:T(8,128)} %bitcast.230), custom_call_target="tpu_custom_call" | custom-call | flops 57344000 | bytes 114688 | tf_op jit(solution)/shard_map/exchange_8/pallas_call | solution.py:129
  214.8 0.9 reduce_sum.169
  215.8 1.4 fusion.80
  218.7 4.5 convolution_convert_fusion.1.refs_0_
  223.2 11.2 %exchange_9.1 = bf16[4,16,5120]{2,1,0:T(8,128)(2,1)} custom-call(bf16[16,5120]{1,0:T(8,128)(2,1)} %convolution_convert_fusion.1.refs_0_), custom_call_target="tpu_custom_call" | custom-call | flops 655360000 | bytes 1310720 | tf_op jit(solution)/shard_map/exchange_9/pallas_call | solution.py:129
  234.4 1.2 convert_reduce_fusion
  235.6 0.8 multiply_reduce_fusion
  237.1 5.0 %exchange_10.1 = f32[2,16,128]{2,1,0:T(8,128)} custom-call(f32[16,128]{1,0:T(8,128)} %broadcast_in_dim.134.refs_0_), custom_call_target="tpu_custom_call" | custom-call | flops 8192000 | bytes 16384 | tf_op jit(solution)/shard_map/exchange_10/pallas_call | solution.py:129
  242.1 1.3 slice_reduce_fusion
  247.1 1.0 bitcast_multiply_fusion.2.refs_0_
  248.0 32.0 %exchange_3.1 = bf16[4,256,1280]{2,1,0:T(8,128)(2,1)} custom-call(bf16[256,1280]{1,0:T(8,128)(2,1)} %bitcast_multiply_fusion.2.refs_0_), custom_call_target="tpu_custom_call" | custom-call | flops 2621440000 | bytes 5242880 | tf_op jit(solution)/shard_map/exchange_3/pallas_call | solution.py:129
  280.1 3.0 copy.242
  283.1 5.9 %convolution_convert_fusion.4 = bf16[256,640]{1,0:T(8,128)(2,1)} fusion(bf16[256,5120]{0,1:T(8,128)(2,1)S(1)} %bitcast.212, bf16[640,5120]{1,0:T(8,128)(2,1)} %param.19), kind=kOutput, calls=%fused_computation.25 | convolution fusion | flops 1677885440 | bytes 9502720 | tf_op jit(solution)/shard_map/dot_general | solution.py:230
  289.0 1.3 reshape.535
  291.2 1.2 convolution_convert_fusion.6
  294.3 0.9 multiply_convert_fusion.1
  295.8 2.1 dynamic-slice_select_fusion
  298.7 2.0 gather_fusion
  300.7 2.2 add_convert_fusion
  302.9 60.6 %all-gather.8.cloned.1.call-done = bf16[2048,896]{1,0:T(8,128)(2,1)} async-done(((bf16[256,896]{1,0:T(8,128)(2,1)}), bf16[2048,896]{1,0:T(8,128)(2,1)}) %all-gather.8.cloned.1.call-update) | async-done | bytes 3670032 | tf_op jit(solution)/shard_map/all_gather | solution.py:278
  363.5 89.1 %all-gather.6.cloned.1.call-done = bf16[2048,2560]{1,0:T(8,128)(2,1)} async-done(((bf16[128,2560]{1,0:T(8,128)(2,1)}), bf16[2048,2560]{1,0:T(8,128)(2,1)}) %all-gather.6.cloned.1.call-update) | async-done | bytes 10485776 | tf_op jit(solution)/shard_map/all_gather | solution.py:203
  452.6 13.8 %fusion.4 = f32[2560,640]{1,0:T(8,128)} fusion(bf16[2048,2560]{1,0:T(8,128)(2,1)} %all-gather.6.cloned.1.call-done, bf16[2048,896]{1,0:T(8,128)(2,1)} %all-gather.8.cloned.1.call-done), kind=kOutput, calls=%fused_computation.14 | convolution fusion | flops 6710886400 | bytes 19660800 | tf_op jit(solution)/shard_map/dot_general | solution.py:280
  466.4 5.0 %fusion.27 = f32[2560,128]{1,0:T(8,128)} fusion(bf16[2048,2560]{1,0:T(8,128)(2,1)S(1)} %copy-done.32, bf16[2048,896]{1,0:T(8,128)(2,1)} %all-gather.8.cloned.1.call-done), kind=kOutput, calls=%fused_computation.58 | convolution fusion | flops 1342177280 | bytes 12320768 | tf_op jit(solution)/shard_map/dot_general | solution.py:280
  471.4 5.2 %fusion.25 = f32[2560,128]{1,0:T(8,128)} fusion(bf16[2048,2560]{1,0:T(8,128)(2,1)S(1)} %copy-done.32, bf16[2048,896]{1,0:T(8,128)(2,1)} %all-gather.8.cloned.1.call-done), kind=kOutput, calls=%fused_computation.56 | convolution fusion | flops 1342177280 | bytes 12320768 | tf_op jit(solution)/shard_map/dot_general | solution.py:280
  (162 shorter events, 19.7 us)
Async XLA Ops:
  8.0 100.4 %copy-start = (bf16[2560,640]{1,0:T(8,128)(2,1)S(1)}, bf16[2560,640]{1,0:T(8,128)(2,1)}, u32[]{:S(2)}) copy-start(bf16[2560,640]{1,0:T(8,128)(2,1)} %param.16) | copy-start | bytes 9830404
  8.0 290.6 %all-gather.4.cloned.1.call-start = ((), (), s32[]{:S(2)}) async-start(), calls=%async_computation.1 | async-start | bytes 1966080 | tf_op jit(solution)/shard_map/all_gather | solution.py:212
  8.8 292.0 %reduce-scatter.2.cloned.1.call-start = ((), (), s32[]{:S(2)}) async-start(), calls=%async_computation.2 | async-start | bytes 3276800 | tf_op jit(solution)/shard_map/reduce_scatter | solution.py:223
  43.2 4.7 copy-start.3
  43.3 5.3 %copy-start.26 = (s32[32]{0:T(128)S(1)}, s32[32]{0:T(128)}, u32[]{:S(2)}) copy-start(s32[32]{0:T(128)} %param.25) | copy-start | bytes 388
  49.0 62.4 %copy-start.30 = (s32[32]{0:T(128)}, s32[32]{0:T(128)S(1)}, u32[]{:S(2)}) copy-start(s32[32]{0:T(128)S(1)} %select_reduce_fusion) | copy-start | bytes 388
  55.2 5.9 %copy-start.14 = (f32[5120]{0:T(1024)S(1)}, f32[5120]{0:T(1024)}, u32[]{:S(2)}) copy-start(f32[5120]{0:T(1024)} %param.15) | copy-start | bytes 61444
  104.5 2.2 copy-start.4
  104.5 3.0 copy-start.5
  108.4 3.7 copy-start.2
  112.0 21.9 %copy-start.28 = (s32[16]{0:T(128)}, s32[16]{0:T(128)S(1)}, u32[]{:S(2)}) copy-start(s32[16]{0:T(128)S(1)} %get-tuple-element.9) | copy-start | bytes 196
  112.0 21.9 %copy-start.25 = (s32[1024]{0:T(1024)}, s32[1024]{0:T(1024)S(1)}, u32[]{:S(2)}) copy-start(s32[1024]{0:T(1024)S(1)} %pad_clamp_fusion.1) | copy-start | bytes 12292
  117.3 21.4 %copy-start.19 = (pred[16,16,16]{1,2,0:T(8,128)(4,1)S(1)}, pred[16,16,16]{1,2,0:T(8,128)(4,1)}, u32[]{:S(2)}) copy-start(pred[16,16,16]{1,2,0:T(8,128)(4,1)} %broadcast_and_fusion) | copy-start | bytes 12292
  138.7 1.9 copy-start.18
  140.6 0.8 copy-start.10
  140.6 0.8 copy-start.16
  141.4 6.9 %copy-start.7 = (bf16[16,5120]{1,0:T(8,128)(2,1)S(1)}, bf16[16,5120]{1,0:T(8,128)(2,1)}, u32[]{:S(2)}) copy-start(bf16[16,5120]{1,0:T(8,128)(2,1)} %param.14) | copy-start | bytes 491524
  141.4 7.0 %copy-start.15 = (f32[5120]{0:T(1024)S(1)}, f32[5120]{0:T(1024)}, u32[]{:S(2)}) copy-start(f32[5120]{0:T(1024)} %param.15) | copy-start | bytes 61444
  148.0 215.5 %all-gather.8.cloned.1.call-start = ((), (), s32[]{:S(2)}) async-start(), calls=%async_computation.4 | async-start | bytes 4128768 | tf_op jit(solution)/shard_map/all_gather | solution.py:278
  196.1 0.7 copy-start.8
  197.6 18.2 %copy-start.23 = (bf16[16,1,128]{2,0,1:T(8,128)(2,1)S(1)}, bf16[16,1,128]{2,0,1:T(8,128)(2,1)}, u32[]{:S(2)}) copy-start(bf16[16,1,128]{2,0,1:T(8,128)(2,1)} %get-tuple-element.19) | copy-start | bytes 12292
  206.7 11.5 %copy-start.22 = (bf16[16,1,128]{2,0,1:T(8,128)(2,1)S(1)}, bf16[16,1,128]{2,0,1:T(8,128)(2,1)}, u32[]{:S(2)}) copy-start(bf16[16,1,128]{2,0,1:T(8,128)(2,1)} %get-tuple-element.16) | copy-start | bytes 12292
  208.3 9.9 %copy-start.6 = (bf16[16,128,128]{2,1,0:T(8,128)(2,1)S(1)}, bf16[16,128,128]{2,1,0:T(8,128)(2,1)}, u32[]{:S(2)}) copy-start(bf16[16,128,128]{2,1,0:T(8,128)(2,1)} %param.21) | copy-start | bytes 1572868
  223.2 12.4 %copy-start.9 = (bf16[16,5120]{1,0:T(8,128)(2,1)S(1)}, bf16[16,5120]{1,0:T(8,128)(2,1)}, u32[]{:S(2)}) copy-start(bf16[16,5120]{1,0:T(8,128)(2,1)} %copy-done.8) | copy-start | bytes 491524
  223.2 12.5 %copy-start.21 = (f32[5120]{0:T(1024)S(1)}, f32[5120]{0:T(1024)}, u32[]{:S(2)}) copy-start(f32[5120]{0:T(1024)} %param.23) | copy-start | bytes 61444
  223.2 23.8 %copy-start.24 = (bf16[16,16]{1,0:T(8,128)(2,1)S(1)}, bf16[16,16]{1,0:T(8,128)(2,1)}, u32[]{:S(2)}) copy-start(bf16[16,16]{1,0:T(8,128)(2,1)} %get-tuple-element.22) | copy-start | bytes 1540
  223.2 23.9 %copy-start.12 = (bf16[16,16,1280]{2,1,0:T(8,128)(2,1)S(1)}, bf16[16,16,1280]{2,1,0:T(8,128)(2,1)}, u32[]{:S(2)}) copy-start(bf16[16,16,1280]{2,1,0:T(8,128)(2,1)} %param.27) | copy-start | bytes 1966084
  283.0 7.3 %copy-start.17 = (f32[16,5,16]{2,1,0:T(8,128)S(1)}, f32[16,5,16]{2,1,0:T(8,128)}, u32[]{:S(2)}) copy-start(f32[16,5,16]{2,1,0:T(8,128)} %copy-done.16) | copy-start | bytes 15364
  283.0 7.3 %copy-start.11 = (f32[16,1,5,16,16]{3,4,2,0,1:T(8,128)S(1)}, f32[16,1,5,16,16]{3,4,2,0,1:T(8,128)}, u32[]{:S(2)}) copy-start(f32[16,1,5,16,16]{3,4,2,0,1:T(8,128)} %copy-done.10) | copy-start | bytes 245764
  283.1 8.1 %copy-start.20 = (pred[16,16,16]{1,2,0:T(8,128)(4,1)S(1)}, pred[16,16,16]{1,2,0:T(8,128)(4,1)}, u32[]{:S(2)}) copy-start(pred[16,16,16]{1,2,0:T(8,128)(4,1)} %broadcast_and_fusion) | copy-start | bytes 12292
  290.4 3.0 copy-start.29
  292.4 1.5 copy-start.13
  293.6 1.9 copy-start.31
  293.9 4.6 copy-start.27
  295.2 157.4 %all-gather.6.cloned.1.call-start = ((), (), s32[]{:S(2)}) async-start(), calls=%async_computation.3 | async-start | bytes 11141120 | tf_op jit(solution)/shard_map/all_gather | solution.py:203
  452.6 13.8 %copy-start.32 = (bf16[2048,2560]{1,0:T(8,128)(2,1)S(1)}, bf16[2048,2560]{1,0:T(8,128)(2,1)}, u32[]{:S(2)}) copy-start(bf16[2048,2560]{1,0:T(8,128)(2,1)} %all-gather.6.cloned.1.call-done) | copy-start | bytes 31457284
  471.4 5.2 %copy-start.1 = (bf16[2560,640]{1,0:T(8,128)(2,1)S(1)}, bf16[2560,640]{1,0:T(8,128)(2,1)}, u32[]{:S(2)}) copy-start(bf16[2560,640]{1,0:T(8,128)(2,1)} %param.16) | copy-start | bytes 9830404
Sparse Core Ops, SparseCore 0:
  10.4 26.9 all-gather.3
  295.3 68.1 all-gather.7
  366.3 86.2 all-gather.5
Sparse Core Ops, SparseCore 1:
  148.1 34.8 reduce-scatter.1
